TPU v7x, 8 devices: a whole 2x2x1 slice. The times are simulated.
8 devices in a mesh: dp: 1 (over z), tp: 2 (over y), ep: 4 (over x, core).
Axes of the slice: x: 2, y: 2, z: 1, core: 2. Of those that a mesh axis runs over, the one named last changes fastest.
Arguments:
- hidden: bfloat16 [2048, 1024], P(('dp', 'ep'))
- k_cache: bfloat16 [2048, 256, 8, 64], P(('dp', 'ep'), None, 'tp')
- v_cache: bfloat16 [2048, 256, 8, 64], P(('dp', 'ep'), None, 'tp')
- lengths: int32 [2048], P(('dp', 'ep'))
- expert_ids: int32 [2048, 8], P(('dp', 'ep'))
- route_gates: float32 [2048, 8], P(('dp', 'ep'))
- norm_gain: float32 [1024], replicated
- w_query: bfloat16 [1024, 1024], P(None, 'tp')
- w_key: bfloat16 [1024, 512], P(None, 'tp')
- w_value: bfloat16 [1024, 512], P(None, 'tp')
- w_out: bfloat16 [1024, 1024], P('tp')
- ws_gate: bfloat16 [1024, 512], P(None, 'tp')
- ws_up: bfloat16 [1024, 512], P(None, 'tp')
- ws_down: bfloat16 [512, 1024], P('tp')
- we_gate: bfloat16 [32, 1024, 512], P(('ep', 'tp'))
- we_up: bfloat16 [32, 1024, 512], P(('ep', 'tp'))
- we_down: bfloat16 [32, 512, 1024], P(('ep', 'tp'))
Outputs:
- output: bfloat16 [2048, 1024], P(('dp', 'ep'))
All inputs are finite; a program needn't handle non-finite values.
Results may differ from a plain program's by a relative error of at most 0.0063324.
Values are sent between devices in bfloat16 or wider.
A program may use at most 1 GiB of HBM per device.

v0:
```python
import jax
import jax.numpy as jnp
from jax import lax
from jax.sharding import PartitionSpec as P

NORM_EPS = 1e-6


def rms_norm(hidden, norm_gain):
    hid_f32 = hidden.astype(jnp.float32)
    inv_rms = lax.rsqrt(jnp.mean(hid_f32 * hid_f32, axis=-1, keepdims=True) + NORM_EPS)
    return (hid_f32 * inv_rms * norm_gain).astype(jnp.bfloat16)


def local_attention(x_norm, k_cache, v_cache, lengths, w_query, w_key, w_value, w_out):
    n_rows, seq_len, kv_local, head_dim = k_cache.shape
    q_local = w_query.shape[1] // head_dim
    group_q = q_local // kv_local
    query_h = jnp.dot(x_norm, w_query, preferred_element_type=jnp.float32).astype(jnp.bfloat16).reshape(n_rows, kv_local, group_q, head_dim)
    key_new = jnp.dot(x_norm, w_key, preferred_element_type=jnp.float32).astype(jnp.bfloat16).reshape(n_rows, kv_local, head_dim)
    value_new = jnp.dot(x_norm, w_value, preferred_element_type=jnp.float32).astype(jnp.bfloat16).reshape(n_rows, kv_local, head_dim)
    score_scale = head_dim ** -0.5
    s_cache = jnp.einsum('bkgd,bskd->bkgs', query_h, k_cache, preferred_element_type=jnp.float32) * score_scale
    valid_pos = jnp.arange(seq_len)[None, :] < lengths[:, None]
    s_cache = jnp.where(valid_pos[:, None, None, :], s_cache, -1e30)
    s_new = jnp.einsum('clhe,cle->clh', query_h, key_new, preferred_element_type=jnp.float32) * score_scale
    peak_score = jnp.maximum(jnp.max(s_cache, axis=-1), s_new)
    p_cache = jnp.exp(s_cache - peak_score[..., None])
    p_new = jnp.exp(s_new - peak_score)
    denom_sum = jnp.sum(p_cache, axis=-1) + p_new
    numer_sum = jnp.einsum('bkgs,bskd->bkgd', p_cache.astype(jnp.bfloat16), v_cache, preferred_element_type=jnp.float32) + p_new[..., None] * value_new.astype(jnp.float32)[:, :, None, :]
    o_flat = (numer_sum / denom_sum[..., None]).astype(jnp.bfloat16).reshape(n_rows, q_local * head_dim)
    return jnp.dot(o_flat, w_out, preferred_element_type=jnp.float32)


def shared_expert(x_norm, ws_gate, ws_up, ws_down):
    gate_s = jnp.dot(x_norm, ws_gate, preferred_element_type=jnp.float32)
    up_s = jnp.dot(x_norm, ws_up, preferred_element_type=jnp.float32)
    return jnp.dot((jax.nn.silu(gate_s) * up_s).astype(jnp.bfloat16), ws_down, preferred_element_type=jnp.float32)


def expert_rows(x_rows, weight, we_gate, we_up, we_down):
    gate_e = jnp.einsum('rd,edf->erf', x_rows, we_gate, preferred_element_type=jnp.float32)
    up_e = jnp.einsum('rd,edf->erf', x_rows, we_up, preferred_element_type=jnp.float32)
    hid_e = (jax.nn.silu(gate_e) * up_e).astype(jnp.bfloat16)
    out_e = jnp.einsum('erf,efd->erd', hid_e, we_down, preferred_element_type=jnp.float32)
    return jnp.einsum('re,erd->rd', weight, out_e)


def solution(mesh):
    tp_size = mesh.shape['tp']
    tok_rows = P(('dp', 'ep'), None)
    cache_spec = P(('dp', 'ep'), None, 'tp', None)
    col_split = P(None, 'tp')
    row_split = P('tp', None)
    exp_split = P(('ep', 'tp'), None, None)
    in_specs = (tok_rows, cache_spec, cache_spec, P(('dp', 'ep')), tok_rows, tok_rows, P(None), col_split, col_split, col_split, row_split, col_split, col_split, row_split, exp_split, exp_split, exp_split)

    def device_body(hidden, k_cache, v_cache, lengths, expert_ids, route_gates, norm_gain, w_query, w_key, w_value, w_out, ws_gate, ws_up, ws_down, we_gate, we_up, we_down):
        half_rows = hidden.shape[0] // 2
        top_k = expert_ids.shape[1]
        n_local = we_gate.shape[0]
        group_experts = n_local * tp_size
        owned_ids = lax.axis_index('tp') * n_local + jnp.arange(n_local)
        n_pairs = half_rows * top_k
        out_halves = []
        for half_idx in range(2):
            row_start = half_idx * half_rows
            h_half = hidden[row_start:row_start + half_rows]
            x_norm = rms_norm(h_half, norm_gain)
            ids_half = expert_ids[row_start:row_start + half_rows].reshape(n_pairs)
            gate_half = route_gates[row_start:row_start + half_rows].reshape(n_pairs)
            dest_group = ids_half // group_experts
            sort_order = jnp.argsort(dest_group * n_pairs + jnp.arange(n_pairs))
            src_tok = sort_order // top_k
            select = (src_tok[:, None] == jnp.arange(half_rows)[None, :]).astype(jnp.bfloat16)
            x_send = jnp.dot(select, x_norm, preferred_element_type=jnp.float32).astype(jnp.bfloat16)
            loc_send = ids_half[sort_order] % group_experts
            gate_send = gate_half[sort_order]
            x_recv = lax.all_to_all(x_send, 'ep', 0, 0, tiled=True)
            loc_recv = lax.all_to_all(loc_send, 'ep', 0, 0, tiled=True)
            gate_recv = lax.all_to_all(gate_send, 'ep', 0, 0, tiled=True)
            weight = jnp.where(loc_recv[:, None] == owned_ids[None, :], gate_recv[:, None], 0.0)
            rows_out = expert_rows(x_recv, weight, we_gate, we_up, we_down).astype(jnp.bfloat16)
            back_rows = lax.all_to_all(rows_out, 'ep', 0, 0, tiled=True)
            routed = jnp.einsum('pt,pd->td', select, back_rows, preferred_element_type=jnp.float32)
            attn_part = local_attention(x_norm, k_cache[row_start:row_start + half_rows], v_cache[row_start:row_start + half_rows], lengths[row_start:row_start + half_rows], w_query, w_key, w_value, w_out)
            shared = shared_expert(x_norm, ws_gate, ws_up, ws_down)
            total_sum = lax.psum(attn_part + shared + routed, 'tp')
            out_halves.append((h_half.astype(jnp.float32) + total_sum).astype(jnp.bfloat16))
        return jnp.concatenate(out_halves, axis=0)

    return jax.shard_map(device_body, mesh=mesh, in_specs=in_specs, out_specs=tok_rows, check_vma=False)
```

profile of v0, /device:TPU:0, one launch (start us, length us, event | category | flops | bytes accessed | tf_op | source)
XLA Modules:
  0.0 522.1 jit_solution(5774281259978162168)
XLA Ops:
  8.6 5.0 sort.31
  13.6 20.6 %gather_fusion.1 = f32[2048]{0:T(1024)} fusion(f32[2048]{0:T(1024)S(1)} %reshape.241, s32[2048]{0:T(1024)S(1)} %get-tuple-element.24), kind=kCustom, calls=%fused_computation.1 | custom fusion | bytes 24576 | tf_op jit(solution)/shard_map/gather | solution.py:79
  38.8 11.8 %gather_fusion = s32[2048]{0:T(1024)S(1)} fusion(s32[2048]{0:T(1024)S(1)} %reshape.240, s32[2048]{0:T(1024)S(1)} %get-tuple-element.24), kind=kCustom, calls=%fused_computation | custom fusion | bytes 24576 | tf_op jit(solution)/shard_map/gather | solution.py:78
  50.9 5.0 sort.32
  64.9 12.7 %fusion.131 = (f32[256,4,2]{2,1,0:T(4,128)S(1)}, f32[256,4,2,256]{3,2,1,0:T(2,128)S(1)}) fusion(bf16[256,4,2,64]{3,2,1,0:T(2,128)(2,1)S(1)} %copy.41, bf16[512,256,4,64]{1,3,2,0:T(8,128)(2,1)} %param.18, pred[256,256]{1,0:T(8,128)(4,1)S(1)} %get-tuple-element.35), kind=kOutput, calls=%fused_computation.171 | convolution fusion | flops 68679680 | bytes 35987456 | tf_op jit(solution)/shard_map/bkgd,bskd->bkgs/dot_general | solution.py:23
  77.9 5.8 %fusion.60 = f32[256,4,2]{2,1,0:T(4,128)S(1)} fusion(f32[256,4,2,256]{3,2,1,0:T(2,128)S(1)} %get-tuple-element.32, f32[256,4,2]{2,1,0:T(4,128)S(1)} %multiply_maximum_fusion), kind=kLoop, calls=%fused_computation.76 | loop fusion | flops 1046528 | bytes 2113536 | tf_op jit(solution)/shard_map/reduce_sum | solution.py:30
  86.2 16.2 %fusion.53 = bf16[256,4,2,64]{3,2,1,0:T(2,128)(2,1)} fusion(bf16[512,256,4,64]{1,3,2,0:T(8,128)(2,1)} %param.19, f32[256,4,2,256]{3,2,1,0:T(2,128)} %copy-done.4, f32[256,4,2]{2,1,0:T(4,128)S(1)} %multiply_maximum_fusion, f32[256,4,2]{2,1,0:T(4,128)S(1)} %get-tuple-element.15, f32[256,4,64]{2,1,0:T(4,128)} %copy.42, f32[256,4,2]{2,1,0:T(4,128)} %get-tuple-element.16), kind=kOutput, calls=%fused_computation.63 | convolution fusion | flops 68681728 | bytes 36978688 | tf_op jit(solution)/shard_map/bkgs,bskd->bkgd/dot_general | solution.py:31
  103.0 11.8 %gather_fusion.2 = s32[2048]{0:T(1024)S(1)} fusion(s32[2048]{0:T(1024)S(1)} %reshape.245, s32[2048]{0:T(1024)S(1)} %get-tuple-element.26), kind=kCustom, calls=%fused_computation.2 | custom fusion | bytes 24576 | tf_op jit(solution)/shard_map/gather | solution.py:78
  118.4 20.6 %gather_fusion.3 = f32[2048]{0:T(1024)} fusion(f32[2048]{0:T(1024)S(1)} %reshape.246, s32[2048]{0:T(1024)S(1)} %get-tuple-element.26), kind=kCustom, calls=%fused_computation.3 | custom fusion | bytes 24576 | tf_op jit(solution)/shard_map/gather | solution.py:79
  157.5 14.4 %fusion.132 = (f32[256,4,2]{2,1,0:T(4,128)S(1)}, f32[256,4,2,256]{3,2,1,0:T(2,128)}) fusion(bf16[256,4,2,64]{3,2,1,0:T(2,128)(2,1)} %copy.33, bf16[512,256,4,64]{1,3,2,0:T(8,128)(2,1)} %param.18, pred[256,256]{1,0:T(8,128)(4,1)S(1)} %get-tuple-element.36), kind=kOutput, calls=%fused_computation.172 | convolution fusion | flops 68679680 | bytes 36249600 | tf_op jit(solution)/shard_map/bkgd,bskd->bkgs/dot_general | solution.py:23
  180.1 5.8 %fusion.58 = f32[256,4,2]{2,1,0:T(4,128)S(1)} fusion(f32[256,4,2,256]{3,2,1,0:T(2,128)S(1)} %copy-done.3, f32[256,4,2]{2,1,0:T(4,128)S(1)} %multiply_maximum_fusion.1), kind=kLoop, calls=%fused_computation.74 | loop fusion | flops 1046528 | bytes 2113536 | tf_op jit(solution)/shard_map/reduce_sum | solution.py:30
  192.9 12.5 %all-to-all-done.6 = bf16[4,512,1024]{2,1,0:T(8,128)(2,1)} async-done(((bf16[4,512,1024]{2,1,0:T(8,128)(2,1)}), bf16[4,512,1024]{2,1,0:T(8,128)(2,1)}, u32[]{:S(2)}, u32[]{:S(2)}) %all-to-all-start.6) | async-done | bytes 4194336 | tf_op jit(solution)/shard_map/all_to_all | solution.py:80
  205.4 5.1 all-to-all-start.2
  210.5 15.3 %fusion.138 = f32[2048,4,512]{2,0,1:T(8,128)} fusion(bf16[2048,1024,1]{1,0,2:T(8,128)(2,1)} %bitcast.35, bf16[4,1024,512]{2,1,0:T(8,128)(2,1)} %param.31), kind=kOutput, calls=%fused_computation.178 | convolution fusion | flops 8589934592 | bytes 25165824 | tf_op jit(solution)/shard_map/rd,edf->erf/dot_general | solution.py:43
  225.8 26.0 %fusion.24 = bf16[4,2048,1024]{2,1,0:T(8,128)(2,1)} fusion(bf16[4,512,1024]{2,1,0:T(8,128)(2,1)} %param.33, f32[2048,4,512]{2,0,1:T(8,128)} %fusion.138, bf16[2048,1024,1]{1,0,2:T(8,128)(2,1)} %bitcast.35, bf16[4,1024,512]{2,1,0:T(8,128)(2,1)} %param.32), kind=kOutput, calls=%fused_computation.32 | convolution fusion | flops 17205035008 | bytes 46137344 | tf_op jit(solution)/shard_map/erf,efd->erd/dot_general | solution.py:46
  251.7 42.0 %fusion = bf16[2048,1,1024]{2,1,0:T(2,128)(2,1)S(1)} fusion(f32[2048,4,1]{1,2,0:T(1,128)S(1)} %bitcast.133, bf16[4,2048,1024]{2,1,0:T(8,128)(2,1)} %fusion.24), kind=kOutput, calls=%fused_computation.4 | convolution fusion | flops 16777216 | bytes 21004288 | tf_op jit(solution)/shard_map/re,erd->rd/dot_general | solution.py:47
  297.4 5.0 all-to-all-start.7
  302.4 15.3 %fusion.135 = f32[2048,4,512]{2,0,1:T(8,128)} fusion(bf16[2048,1024,1]{1,0,2:T(8,128)(2,1)} %bitcast.14, bf16[4,1024,512]{2,1,0:T(8,128)(2,1)} %param.31), kind=kOutput, calls=%fused_computation.175 | convolution fusion | flops 8589934592 | bytes 25165824 | tf_op jit(solution)/shard_map/rd,edf->erf/dot_general | solution.py:43
  317.7 26.0 %fusion.20 = bf16[4,2048,1024]{2,1,0:T(8,128)(2,1)} fusion(bf16[4,512,1024]{2,1,0:T(8,128)(2,1)} %param.33, f32[2048,4,512]{2,0,1:T(8,128)} %fusion.135, bf16[2048,1024,1]{1,0,2:T(8,128)(2,1)} %bitcast.14, bf16[4,1024,512]{2,1,0:T(8,128)(2,1)} %param.32), kind=kOutput, calls=%fused_computation.30 | convolution fusion | flops 17205035008 | bytes 46137344 | tf_op jit(solution)/shard_map/erf,efd->erd/dot_general | solution.py:46
  343.8 41.8 %fusion.2 = bf16[2048,1,1024]{2,1,0:T(2,128)(2,1)S(1)} fusion(f32[2048,4,1]{1,2,0:T(1,128)S(1)} %bitcast.132, bf16[4,2048,1024]{2,1,0:T(8,128)(2,1)} %fusion.20), kind=kOutput, calls=%fused_computation.6 | convolution fusion | flops 16777216 | bytes 21004288 | tf_op jit(solution)/shard_map/re,erd->rd/dot_general | solution.py:47
  389.3 5.0 all-to-all-start.3
  394.4 16.5 %fusion.44 = bf16[256,4,2,64]{3,2,1,0:T(2,128)(2,1)} fusion(bf16[512,256,4,64]{1,3,2,0:T(8,128)(2,1)} %param.19, f32[256,4,2,256]{3,2,1,0:T(2,128)} %get-tuple-element.34, f32[256,4,2]{2,1,0:T(4,128)S(1)} %copy-done.6, f32[256,4,2]{2,1,0:T(4,128)S(1)} %copy-done.9, f32[256,4,64]{2,1,0:T(4,128)} %copy.34, f32[256,4,2]{2,1,0:T(4,128)} %get-tuple-element.14), kind=kOutput, calls=%fused_computation.60 | convolution fusion | flops 68681728 | bytes 36978688 | tf_op jit(solution)/shard_map/bkgs,bskd->bkgd/dot_general | solution.py:31
  423.3 18.9 %all-to-all-done.3 = bf16[4,512,1024]{2,1,0:T(8,128)(2,1)} async-done(((bf16[4,512,1024]{2,1,0:T(8,128)(2,1)}), bf16[4,512,1024]{2,1,0:T(8,128)(2,1)}, u32[]{:S(2)}, u32[]{:S(2)}) %all-to-all-start.3) | async-done | bytes 4194336 | tf_op jit(solution)/shard_map/all_to_all | solution.py:85
  454.2 57.8 %all-reduce.3.cloned.1.call-done = (f32[256,1024]{1,0:T(8,128)}, f32[256,1024]{1,0:T(8,128)}) async-done(((f32[256,1024]{1,0:T(8,128)}, f32[256,1024]{1,0:T(8,128)}), (f32[256,1024]{1,0:T(8,128)}, f32[256,1024]{1,0:T(8,128)})) %all-reduce.3.cloned.1.call-update) | async-done | bytes 2097168 | tf_op jit(solution)/shard_map/psum | solution.py:89
  (128 shorter events, 90.8 us)
Async XLA Ops:
  6.5 409.9 %copy-start = (bf16[512,1024]{1,0:T(8,128)(2,1)S(1)}, bf16[512,1024]{1,0:T(8,128)(2,1)}, u32[]{:S(2)}) copy-start(bf16[512,1024]{1,0:T(8,128)(2,1)} %param.27) | copy-start | bytes 3145732
  13.6 173.6 %copy-start.12 = (s32[2048]{0:T(1024)}, s32[2048]{0:T(1024)S(1)}, u32[]{:S(2)}) copy-start(s32[2048]{0:T(1024)S(1)} %get-tuple-element.23) | copy-start | bytes 24580
  34.2 80.7 %all-to-all-start.1 = ((f32[4,512,1]{1,2,0:T(1,128)}), f32[4,512,1]{1,2,0:T(1,128)S(1)}, u32[]{:S(2)}, u32[]{:S(2)}) async-start(f32[4,512,1]{1,2,0:T(1,128)} %bitcast.8), calls=%async_computation.1 | async-start | bytes 16384 | tf_op jit(solution)/shard_map/all_to_all | solution.py:82
  38.8 17.1 %copy-start.1 = (bf16[512,1024]{1,0:T(8,128)(2,1)S(1)}, bf16[512,1024]{1,0:T(8,128)(2,1)}, u32[]{:S(2)}) copy-start(bf16[512,1024]{1,0:T(8,128)(2,1)} %param.17) | copy-start | bytes 3145732
  38.8 17.4 %copy-start.16 = (f32[1024]{0:T(1024)S(1)}, f32[1024]{0:T(1024)}, u32[]{:S(2)}) copy-start(f32[1024]{0:T(1024)} %param.23) | copy-start | bytes 12292
  56.2 28.5 %copy-start.18 = (f32[256]{0:T(256)}, f32[256]{0:T(256)S(1)}, u32[]{:S(2)}) copy-start(f32[256]{0:T(256)S(1)} %add_rsqrt_fusion) | copy-start | bytes 3076
  77.7 7.6 %copy-start.4 = (f32[256,4,2,256]{3,2,1,0:T(2,128)}, f32[256,4,2,256]{3,2,1,0:T(2,128)S(1)}, u32[]{:S(2)}) copy-start(f32[256,4,2,256]{3,2,1,0:T(2,128)S(1)} %get-tuple-element.32) | copy-start | bytes 6291460
  114.9 24.1 %all-to-all-start = ((s32[4,512,1]{1,2,0:T(1,128)}), s32[4,512,1]{1,2,0:T(1,128)S(1)}, u32[]{:S(2)}, u32[]{:S(2)}) async-start(s32[4,512,1]{1,2,0:T(1,128)} %copy.37), calls=%async_computation | async-start | bytes 16384 | tf_op jit(solution)/shard_map/all_to_all | solution.py:81
  139.0 6.9 %all-to-all-start.5 = ((f32[4,512,1]{1,2,0:T(1,128)}), f32[4,512,1]{1,2,0:T(1,128)S(1)}, u32[]{:S(2)}, u32[]{:S(2)}) async-start(f32[4,512,1]{1,2,0:T(1,128)} %bitcast.29), calls=%async_computation.5 | async-start | bytes 16384 | tf_op jit(solution)/shard_map/all_to_all | solution.py:82
  142.3 45.0 %copy-start.20 = (f32[256]{0:T(256)}, f32[256]{0:T(256)S(1)}, u32[]{:S(2)}) copy-start(f32[256]{0:T(256)S(1)} %add_rsqrt_fusion.1) | copy-start | bytes 3076
  145.9 6.8 %all-to-all-start.4 = ((s32[4,512,1]{1,2,0:T(1,128)}), s32[4,512,1]{1,2,0:T(1,128)S(1)}, u32[]{:S(2)}, u32[]{:S(2)}) async-start(s32[4,512,1]{1,2,0:T(1,128)} %copy.45), calls=%async_computation.4 | async-start | bytes 16384 | tf_op jit(solution)/shard_map/all_to_all | solution.py:81
  152.6 52.8 %all-to-all-start.6 = ((bf16[4,512,1024]{2,1,0:T(8,128)(2,1)}), bf16[4,512,1024]{2,1,0:T(8,128)(2,1)}, u32[]{:S(2)}, u32[]{:S(2)}) async-start(bf16[4,512,1024]{2,1,0:T(8,128)(2,1)} %bitcast.122), calls=%async_computation.6 | async-start | bytes 8388608 | tf_op jit(solution)/shard_map/all_to_all | solution.py:80
  157.5 14.4 %copy-start.10 = (bf16[256,4,2,64]{3,2,1,0:T(2,128)(2,1)S(1)}, bf16[256,4,2,64]{3,2,1,0:T(2,128)(2,1)}, u32[]{:S(2)}) copy-start(bf16[256,4,2,64]{3,2,1,0:T(2,128)(2,1)} %fusion.53) | copy-start | bytes 786436
  180.1 7.2 %copy-start.5 = (f32[256,4,2]{2,1,0:T(4,128)}, f32[256,4,2]{2,1,0:T(4,128)S(1)}, u32[]{:S(2)}) copy-start(f32[256,4,2]{2,1,0:T(4,128)S(1)} %multiply_maximum_fusion.1) | copy-start | bytes 24580
  205.4 92.0 %all-to-all-start.2 = ((bf16[4,512,1024]{2,1,0:T(8,128)(2,1)}), bf16[4,512,1024]{2,1,0:T(8,128)(2,1)}, u32[]{:S(2)}, u32[]{:S(2)}) async-start(bf16[4,512,1024]{2,1,0:T(8,128)(2,1)} %bitcast.123), calls=%async_computation.2 | async-start | bytes 8388608 | tf_op jit(solution)/shard_map/all_to_all | solution.py:80
  297.4 91.9 %all-to-all-start.7 = ((bf16[4,512,1024]{2,1,0:T(8,128)(2,1)}), bf16[4,512,1024]{2,1,0:T(8,128)(2,1)}, u32[]{:S(2)}, u32[]{:S(2)}) async-start(bf16[4,512,1024]{2,1,0:T(8,128)(2,1)} %bitcast.125), calls=%async_computation.7 | async-start | bytes 8388608 | tf_op jit(solution)/shard_map/all_to_all | solution.py:85
  317.7 26.1 %copy-start.8 = (f32[2048,4]{1,0:T(8,128)S(1)}, f32[2048,4]{1,0:T(8,128)}, u32[]{:S(2)}) copy-start(f32[2048,4]{1,0:T(8,128)} %get-tuple-element.29) | copy-start | bytes 98308
  389.3 52.9 %all-to-all-start.3 = ((bf16[4,512,1024]{2,1,0:T(8,128)(2,1)}), bf16[4,512,1024]{2,1,0:T(8,128)(2,1)}, u32[]{:S(2)}, u32[]{:S(2)}) async-start(bf16[4,512,1024]{2,1,0:T(8,128)(2,1)} %bitcast.124), calls=%async_computation.3 | async-start | bytes 8388608 | tf_op jit(solution)/shard_map/all_to_all | solution.py:85
  394.3 117.6 %all-reduce.3.cloned.1.call-start = ((), (), s32[]{:S(2)}) async-start(), calls=%async_computation.8 | async-start | bytes 4194304 | tf_op jit(solution)/shard_map/psum | solution.py:89
  394.4 17.8 %copy-start.2 = (bf16[512,1024]{1,0:T(8,128)(2,1)S(1)}, bf16[512,1024]{1,0:T(8,128)(2,1)}, u32[]{:S(2)}) copy-start(bf16[512,1024]{1,0:T(8,128)(2,1)} %param.17) | copy-start | bytes 3145732
  394.4 17.8 %copy-start.17 = (f32[1024]{0:T(1024)S(1)}, f32[1024]{0:T(1024)}, u32[]{:S(2)}) copy-start(f32[1024]{0:T(1024)} %param.23) | copy-start | bytes 12292
  394.4 17.8 %copy-start.19 = (f32[256]{0:T(256)S(1)}, f32[256]{0:T(256)}, u32[]{:S(2)}) copy-start(f32[256]{0:T(256)} %copy-done.18) | copy-start | bytes 3076
  394.4 19.9 %copy-start.21 = (f32[256]{0:T(256)S(1)}, f32[256]{0:T(256)}, u32[]{:S(2)}) copy-start(f32[256]{0:T(256)} %copy-done.20) | copy-start | bytes 3076
  418.4 23.7 %copy-start.13 = (s32[2048]{0:T(1024)S(1)}, s32[2048]{0:T(1024)}, u32[]{:S(2)}) copy-start(s32[2048]{0:T(1024)} %copy-done.12) | copy-start | bytes 24580
  (10 other events, 45.1 us)
Sparse Core Ops, SparseCore 0:
  454.3 57.6 all-reduce.2
where the time goes:
time: 531 us; the launch traced here: 522 us
  matrix products  267 us (50%)
  waiting for transfers between devices  92.8 us (17%)
  local copies, waits for them, and re-layouts  83.8 us (16%)
  starting transfers between devices  34.4 us (6%)
  other arithmetic  29.4 us (6%)
  between operations  14.4 us (3%)
    dot_general x2, matrix products, expert_rows(): return jnp.einsum('re,erd->rd', weight, out_e)  83.8 us
    psum x1, waiting for transfers between devices, device_body(): total_sum = lax.psum(attn_part + shared + routed, 'tp')  57.8 us
    dot_general x2, matrix products, expert_rows(): jnp.einsum('erf,efd->erd', hid_e, we_down, preferred_element_type=jnp.flo...  52 us
    gather x2, local copies, waits for them, and re-layouts, device_body(): gate_send = gate_half[sort_order]  41.1 us
    dot_general x2, matrix products, local_attention(): jnp.einsum('bkgs,bskd->bkgd', p_cache.astype(jnp.bfloat16), v_cache, pref...  32.7 us
    dot_general x2, matrix products, expert_rows(): jnp.einsum('rd,edf->erf', x_rows, we_gate, preferred_element_type=jnp.flo...  30.6 us
    dot_general x2, matrix products, local_attention(): jnp.einsum('bkgd,bskd->bkgs', query_h, k_cache, preferred_element_type=jn...  27.1 us
    gather x4, local copies, waits for them, and re-layouts, device_body(): loc_send = ids_half[sort_order] % group_experts  23.6 us
  transfers between devices with their start and end apart: 9, of which 5 were waited for; matrix products, arithmetic and copies ran while one was open for 65% of the time, Pallas kernels for 0%

commit v1 on v0

v1 whole, which is shorter than its diff:
```python
import functools

import jax
import jax.numpy as jnp
from jax import lax
from jax.experimental import pallas as pl
from jax.experimental.pallas import tpu as pltpu
from jax.sharding import PartitionSpec as P

NORM_EPS = 1e-6
F32 = jnp.float32
BF16 = jnp.bfloat16
MESH = pl.DeviceIdType.MESH

BLK = 16
SLOTS = 4
CHUNK = 64
HEAD_BLOCKS = 8


def layer_kernel(
    h_ref, ids_ref, gates_ref, lens_ref, gain_ref, k_hbm, v_hbm, wq_hbm, wk_hbm, wv_hbm, wo_hbm, wsg_hbm, wsu_hbm, wsd_hbm,
    weg_hbm, weu_hbm, wed_hbm,
    out_hbm,
    wq, wk, wv, wo, wsg, wsu, wsd, weg, weu, wed, kbuf, vbuf,
    h_in, ids_in, gates_in, xs, aug, oflat, acc, part, cwb,
    psend, precv, dsend, drecv, xsend, xrecv, ysend, yrecv, obuf,
    wsem, wosem, esem, ksem, vsem, hs_send, hs_recv, p_send, p_recv, d_send, d_recv, x_send, x_recv, y_send, y_recv, osem,
):
    tp = lax.axis_index("tp")
    ep = lax.axis_index("ep")
    dp = lax.axis_index("dp")
    core = lax.rem(ep, 2)
    chip = ep // 2
    partner = (dp, tp, 2 * chip + 1 - core)
    xnbr = (dp, tp, 2 * (1 - chip) + core)
    ynbr = (dp, 1 - tp, ep)

    rows = h_ref.shape[0]
    n_blocks = rows // BLK
    n_chunks = rows // CHUNK
    kv_width = wk.shape[1]
    n_local = weg.shape[0]
    n_heads = wq.shape[1] // 64
    seq_len = kbuf.shape[3]

    small = [(wq_hbm, wq), (wk_hbm, wk), (wv_hbm, wv), (wsg_hbm, wsg), (wsu_hbm, wsu), (wsd_hbm, wsd)]
    small_copies = [pltpu.make_async_copy(s, d, wsem.at[i]) for i, (s, d) in enumerate(small)]
    for c in small_copies:
        c.start()
    barrier = pltpu.get_barrier_semaphore()
    for dev in (partner, xnbr, ynbr):
        pl.semaphore_signal(barrier, inc=1, device_id=dev, device_id_type=MESH)
    big_copies = [pltpu.make_async_copy(s, d, esem.at[i]) for i, (s, d) in enumerate(((weg_hbm, weg), (weu_hbm, weu), (wed_hbm, wed)))]
    for c in big_copies:
        c.start()
    pl.semaphore_wait(barrier, 3)

    def remote(src, dst, ssem, rsem, dev):
        return pltpu.make_async_remote_copy(src_ref=src, dst_ref=dst, send_sem=ssem, recv_sem=rsem, device_id=dev, device_id_type=MESH)

    def token_copies(srcs, slot, dev):
        dsts = (h_in.at[slot], ids_in.at[slot], gates_in.at[slot])
        return [remote(s, d, hs_send.at[slot, i], hs_recv.at[slot, i], dev) for i, (s, d) in enumerate(zip(srcs, dsts))]

    own = (h_ref, ids_ref, gates_ref)
    to_partner = token_copies(own, 0, partner)
    to_xnbr = token_copies(own, 1, xnbr)
    forward = token_copies((h_in.at[1], ids_in.at[1], gates_in.at[1]), 2, partner)
    for c in to_xnbr + to_partner:
        c.start()

    wo_copies = []
    for i in range(n_heads):
        dst_row = (i % 2) * kv_width + (i // 2) * 64
        wo_copies.append(pltpu.make_async_copy(wo_hbm.at[pl.ds(i * 64, 64), :], wo.at[pl.ds(dst_row, 64), :], wosem.at[i]))

    def kv_copies(b, slot):
        start = pl.multiple_of(b * BLK, BLK)
        return (
            pltpu.make_async_copy(k_hbm.at[pl.ds(start, BLK)], kbuf.at[slot], ksem.at[slot]),
            pltpu.make_async_copy(v_hbm.at[pl.ds(start, BLK)], vbuf.at[slot], vsem.at[slot]),
        )

    def normalize(src):
        @pl.loop(0, rows // 64)
        def _(i):
            r = pl.ds(pl.multiple_of(i * 64, 64), 64)
            hf = src[r, :].astype(F32)
            inv = lax.rsqrt(jnp.mean(hf * hf, axis=1, keepdims=True) + NORM_EPS)
            xs[r, :] = (hf * inv * gain_ref[...]).astype(BF16)

    def gate_weights(ids, gates):
        first = ep * (2 * n_local) + tp * n_local
        expert = first + lax.broadcasted_iota(jnp.int32, (8, rows), 0)
        total = jnp.zeros((8, rows), F32)
        for j in range(ids.shape[0]):
            total += jnp.where(ids[j : j + 1, :] == expert, gates[j : j + 1, :], 0.0)
        cols = total.T
        for e in range(n_local):
            cwb[e] = jnp.broadcast_to(cols[:, e : e + 1], (rows, 128))

    half = rows // 2

    def experts(dst, first):
        @pl.loop(0, n_local)
        def _(e):
            for m in range(2):
                r = pl.ds(m * half, half)
                x = xs[r, :]
                gate = jnp.dot(x, weg[e], preferred_element_type=F32)
                up = jnp.dot(x, weu[e], preferred_element_type=F32)
                hid = (gate * jax.nn.sigmoid(gate) * up).astype(BF16)
                y = jnp.dot(hid, wed[e], preferred_element_type=F32)
                w = jnp.tile(cwb[e, r, :], (1, y.shape[1] // 128))
                if first:
                    @pl.when(e == 0)
                    def _():
                        dst[r, :] = w * y

                    @pl.when(e > 0)
                    def _():
                        dst[r, :] += w * y
                else:
                    dst[r, :] += w * y

    normalize(h_ref)
    for c in small_copies:
        c.wait()
    for c in wo_copies:
        c.start()
    for b in range(SLOTS):
        for c in kv_copies(b, b):
            c.start()

    col = lax.broadcasted_iota(jnp.int32, (n_heads * 64, n_heads * 64), 1)
    row = lax.broadcasted_iota(jnp.int32, (n_heads * 64, n_heads * 64), 0)
    src_row = ((lax.rem(col, kv_width) // 64) * 2 + col // kv_width) * 64 + lax.rem(col, 64)
    perm = (row == src_row).astype(F32).astype(BF16)
    lens = jnp.broadcast_to(lens_ref[...], (8, rows)).astype(F32).T
    q_w = n_heads * 64
    for m in range(2):
        r = pl.ds(m * half, half)
        x = xs[r, :]
        q = jnp.dot(x, wq[...], preferred_element_type=F32).astype(BF16)
        aug[r, 0:q_w] = jnp.dot(q, perm, preferred_element_type=F32).astype(BF16)
        aug[r, q_w : q_w + kv_width] = jnp.dot(x, wk[...], preferred_element_type=F32).astype(BF16)
        aug[r, q_w + kv_width : q_w + 2 * kv_width] = jnp.dot(x, wv[...], preferred_element_type=F32).astype(BF16)
        aug[r, q_w + 2 * kv_width : q_w + 2 * kv_width + 128] = jnp.broadcast_to(lens[m * half : (m + 1) * half, 0:1], (half, 128)).astype(BF16)
        gate = jnp.dot(x, wsg[...], preferred_element_type=F32)
        up = jnp.dot(x, wsu[...], preferred_element_type=F32)
        hid = (gate * jax.nn.sigmoid(gate) * up).astype(BF16)
        acc[r, :] = jnp.dot(hid, wsd[...], preferred_element_type=F32)

    gate_weights(ids_ref[...], gates_ref[...])
    for c in big_copies:
        c.wait()
    experts(acc, False)

    def wait_recv(copies):
        for c in copies:
            c.wait_recv()

    wait_recv(to_partner)
    normalize(h_in.at[0])
    gate_weights(ids_in[0], gates_in[0])
    experts(part, True)
    psend[...] = part[...].astype(BF16)
    partner_part = remote(psend, precv, p_send.at[0], p_recv.at[0], partner)
    partner_part.start()

    R8 = BLK * n_heads
    n_pairs = BLK // 2

    def attend(b):
        slot = lax.rem(b, SLOTS)
        for c in kv_copies(b, slot):
            c.wait()
        t = pl.ds(pl.multiple_of(b * BLK, BLK), BLK)
        rep = (lax.broadcasted_iota(jnp.int32, (R8, BLK), 0) // n_heads == lax.broadcasted_iota(jnp.int32, (R8, BLK), 1)).astype(F32).astype(BF16)
        full = jnp.dot(rep, aug[t, :], preferred_element_type=F32)
        r_i = lax.broadcasted_iota(jnp.int32, (R8, kv_width), 0)
        c_i = lax.broadcasted_iota(jnp.int32, (R8, kv_width), 1)
        own_head = lax.rem(r_i, n_heads) // 2 == c_i // 64
        even = lax.rem(r_i, 2) == 0
        qf = jnp.where(own_head, jnp.where(even, full[:, 0:kv_width], full[:, kv_width : 2 * kv_width]), 0.0)
        kn = full[:, q_w : q_w + kv_width]
        vn = full[:, q_w + kv_width : q_w + 2 * kv_width]
        ln = full[:, q_w + 2 * kv_width : q_w + 2 * kv_width + 128]
        qb = qf.astype(BF16)
        s_new = jnp.sum(qf * kn, axis=1, keepdims=True) * 0.125
        parts = []
        for p in range(n_pairs):
            lhs = qb[16 * p : 16 * p + 16]
            parts.append(jnp.dot(lhs, kbuf[slot, 2 * p], preferred_element_type=F32)[0:8])
            parts.append(jnp.dot(lhs, kbuf[slot, 2 * p + 1], preferred_element_type=F32)[8:16])
        s = jnp.concatenate(parts, axis=0) * 0.125
        pos = lax.broadcasted_iota(jnp.int32, (R8, seq_len), 1).astype(F32)
        s = jnp.where(pos < jnp.tile(ln, (1, seq_len // 128)), s, -1e30)
        top = jnp.maximum(jnp.max(s, axis=1, keepdims=True), s_new)
        w = jnp.exp(s - top)
        w_new = jnp.exp(s_new - top)
        den = jnp.sum(w, axis=1, keepdims=True) + w_new
        wb = w.astype(BF16)
        parts = []
        nt = (((1,), (1,)), ((), ()))
        for p in range(n_pairs):
            lhs = wb[16 * p : 16 * p + 16]
            parts.append(lax.dot_general(lhs, vbuf[slot, 2 * p], nt, preferred_element_type=F32)[0:8])
            parts.append(lax.dot_general(lhs, vbuf[slot, 2 * p + 1], nt, preferred_element_type=F32)[8:16])
        num = jnp.concatenate(parts, axis=0) + w_new * vn
        o = jnp.where(own_head, num / den, 0.0).astype(BF16)
        g_r = lax.broadcasted_iota(jnp.int32, (2 * BLK, R8), 0)
        g_c = lax.broadcasted_iota(jnp.int32, (2 * BLK, R8), 1)
        fold = ((g_c // n_heads == lax.rem(g_r, BLK)) & (lax.rem(g_c, 2) == g_r // BLK)).astype(F32).astype(BF16)
        folded = jnp.dot(fold, o, preferred_element_type=F32).astype(BF16)
        oflat[t, 0:kv_width] = folded[0:BLK]
        oflat[t, kv_width : 2 * kv_width] = folded[BLK : 2 * BLK]

    def attend_and_refill(b):
        attend(b)

        @pl.when(b + SLOTS < n_blocks)
        def _():
            for c in kv_copies(b + SLOTS, lax.rem(b, SLOTS)):
                c.start()

    @pl.loop(0, HEAD_BLOCKS)
    def _(b):
        attend_and_refill(b)

    wait_recv(to_xnbr)
    for c in forward:
        c.start()
    normalize(h_in.at[1])
    gate_weights(ids_in[1], gates_in[1])
    experts(part, True)
    partner_part.wait_recv()

    wait_recv(forward)
    normalize(h_in.at[2])
    gate_weights(ids_in[2], gates_in[2])

    @pl.loop(0, n_chunks)
    def _(c):
        r = pl.ds(pl.multiple_of(c * CHUNK, CHUNK), CHUNK)
        acc[r, :] += precv[r, :].astype(F32)
        xpart = part[r, :]
        obuf[r, :] = xpart

    experts(part, True)
    dsend[...] = part[...].astype(BF16)
    diag_part = remote(dsend, drecv, d_send.at[0], d_recv.at[0], partner)
    diag_part.start()
    diag_part.wait_recv()

    def chunk_copy(src, dst, ssem, rsem, c, dev):
        r = pl.ds(pl.multiple_of(c * CHUNK, CHUNK), CHUNK)
        return remote(src.at[r, :], dst.at[r, :], ssem.at[c], rsem.at[c], dev)

    @pl.loop(0, n_chunks)
    def _(c):
        r = pl.ds(pl.multiple_of(c * CHUNK, CHUNK), CHUNK)
        xsend[r, :] = (obuf[r, :] + drecv[r, :].astype(F32)).astype(BF16)
        chunk_copy(xsend, xrecv, x_send, x_recv, c, xnbr).start()

    for c in wo_copies:
        c.wait()

    def finish(c):
        r = pl.ds(pl.multiple_of(c * CHUNK, CHUNK), CHUNK)
        chunk_copy(ysend, yrecv, y_send, y_recv, c, ynbr).wait_recv()
        both = ysend[r, :].astype(F32) + yrecv[r, :].astype(F32)
        xs[r, :] = (h_ref[r, :].astype(F32) + both).astype(BF16)
        pltpu.make_async_copy(xs.at[r, :], out_hbm.at[r, :], osem.at[c]).start()

    per_chunk = (n_blocks - HEAD_BLOCKS) // n_chunks

    @pl.loop(0, n_chunks)
    def _(c):
        @pl.loop(0, per_chunk)
        def _(i):
            attend_and_refill(HEAD_BLOCKS + c * per_chunk + i)

        r = pl.ds(pl.multiple_of(c * CHUNK, CHUNK), CHUNK)
        attn = jnp.dot(oflat[r, :], wo[...], preferred_element_type=F32)
        chunk_copy(xsend, xrecv, x_send, x_recv, c, xnbr).wait_recv()
        ysend[r, :] = (acc[r, :] + attn + xrecv[r, :].astype(F32)).astype(BF16)
        chunk_copy(ysend, yrecv, y_send, y_recv, c, ynbr).start()

        @pl.when(c > 0)
        def _():
            finish(c - 1)

    finish(n_chunks - 1)

    for c in to_partner + to_xnbr + forward + [partner_part, diag_part]:
        c.wait_send()

    @pl.loop(0, n_chunks)
    def _(c):
        r = pl.ds(pl.multiple_of(c * CHUNK, CHUNK), CHUNK)
        chunk_copy(xsend, xrecv, x_send, x_recv, c, xnbr).wait_send()
        chunk_copy(ysend, yrecv, y_send, y_recv, c, ynbr).wait_send()
        pltpu.make_async_copy(xs.at[r, :], out_hbm.at[r, :], osem.at[c]).wait()


def solution(mesh):
    tok_rows = P(("dp", "ep"), None)
    cache_spec = P(("dp", "ep"), None, "tp", None)
    col_split = P(None, "tp")
    row_split = P("tp", None)
    exp_split = P(("ep", "tp"), None, None)
    in_specs = (tok_rows, cache_spec, cache_spec, P(("dp", "ep")), tok_rows, tok_rows, P(None), col_split, col_split, col_split, row_split, col_split, col_split, row_split, exp_split, exp_split, exp_split)

    def device_body(hidden, k_cache, v_cache, lengths, expert_ids, route_gates, norm_gain, w_query, w_key, w_value, w_out, ws_gate, ws_up, ws_down, we_gate, we_up, we_down):
        rows, width = hidden.shape
        seq_len, kv_local, head_dim = k_cache.shape[1:]
        kv_width = kv_local * head_dim
        top_k = expert_ids.shape[1]
        k_t = k_cache.transpose(0, 2, 3, 1).reshape(rows, kv_width, seq_len)
        v_t = v_cache.transpose(0, 2, 3, 1).reshape(rows, kv_width, seq_len)
        n_chunks = rows // CHUNK
        q_w = w_query.shape[1]
        dma = pltpu.SemaphoreType.DMA
        vmem = pltpu.VMEM
        scratch = [
            vmem(w_query.shape, BF16), vmem(w_key.shape, BF16), vmem(w_value.shape, BF16), vmem(w_out.shape, BF16),
            vmem(ws_gate.shape, BF16), vmem(ws_up.shape, BF16), vmem(ws_down.shape, BF16),
            vmem(we_gate.shape, BF16), vmem(we_up.shape, BF16), vmem(we_down.shape, BF16),
            vmem((SLOTS, BLK, kv_width, seq_len), BF16), vmem((SLOTS, BLK, kv_width, seq_len), BF16),
            vmem((3, rows, width), BF16), vmem((3, top_k, rows), jnp.int32), vmem((3, top_k, rows), F32),
            vmem((rows, width), BF16), vmem((rows, q_w + 2 * kv_width + 128), BF16), vmem((rows, q_w), BF16),
            vmem((rows, width), F32), vmem((rows, width), F32), vmem((we_gate.shape[0], rows, 128), F32),
            vmem((rows, width), BF16), vmem((rows, width), BF16), vmem((rows, width), BF16), vmem((rows, width), BF16),
            vmem((rows, width), BF16), vmem((rows, width), BF16), vmem((rows, width), BF16), vmem((rows, width), BF16),
            vmem((rows, width), F32),
            dma((6,)), dma((q_w // head_dim,)), dma((3,)), dma((SLOTS,)), dma((SLOTS,)),
            dma((3, 3)), dma((3, 3)), dma((1,)), dma((1,)), dma((1,)), dma((1,)),
            dma((n_chunks,)), dma((n_chunks,)), dma((n_chunks,)), dma((n_chunks,)), dma((n_chunks,)),
        ]
        in_vmem = pl.BlockSpec(memory_space=pltpu.VMEM)
        anywhere = pl.BlockSpec(memory_space=pl.ANY)
        return pl.pallas_call(
            layer_kernel,
            out_shape=jax.ShapeDtypeStruct((rows, width), BF16),
            in_specs=[in_vmem] * 5 + [anywhere] * 12,
            out_specs=anywhere,
            scratch_shapes=scratch,
            compiler_params=pltpu.CompilerParams(collective_id=0, has_side_effects=True, vmem_limit_bytes=67043328),
            name="moe_layer",
        )(hidden, expert_ids.T, route_gates.T, lengths.reshape(1, rows), norm_gain.reshape(1, width), k_t, v_t, w_query, w_key, w_value, w_out, ws_gate, ws_up, ws_down, we_gate, we_up, we_down)

    return jax.shard_map(device_body, mesh=mesh, in_specs=in_specs, out_specs=tok_rows, check_vma=False)
```

time: 531 us -> 104 us (0.20); the launches traced: 522 us -> 103 us
  matrix products: 267 us -> 0 us
  Pallas kernels: 0 us -> 101 us
  waiting for transfers between devices: 92.8 us -> 0 us
  local copies, waits for them, and re-layouts: 83.8 us -> 2.26 us
  starting transfers between devices: 34.4 us -> 0 us
  other arithmetic: 29.4 us -> 0 us
  between operations: 14.4 us -> 0.01 us
    dot_general x28 -> x0, matrix products: 267 us -> none  [the longest x2 83.8 us: expert_rows(): return jnp.einsum('re,erd->rd', weight, out_e)]
    pallas_call x0 -> x1, Pallas kernels: none -> 101 us  [device_body(): pl.pallas_call(layer_kernel, out_shape=jax.ShapeDtypeStruct((rows, width)...]
    gather x6 -> x0, local copies, waits for them, and re-layouts: 64.7 us -> none  [the longest x2 41.1 us: device_body(): gate_send = gate_half[sort_order]]
    psum x1 -> x0, waiting for transfers between devices: 57.8 us -> none  [device_body(): total_sum = lax.psum(attn_part + shared + routed, 'tp')]
    all_to_all x8 -> x0, waiting for transfers between devices: 35 us -> none  [the longest x2 18.9 us: device_body(): back_rows = lax.all_to_all(rows_out, 'ep', 0, 0, tiled=True)]
    all_to_all x8 -> x0, starting transfers between devices: 34.4 us -> none  [the longest x2 10 us: device_body(): back_rows = lax.all_to_all(rows_out, 'ep', 0, 0, tiled=True)]
    reduce_sum x3 -> x0, other arithmetic: 11.9 us -> none  [the longest x2 11.6 us: local_attention(): denom_sum = jnp.sum(p_cache, axis=-1) + p_new]
    sort x2 -> x0, other arithmetic: 10.1 us -> none  [device_body(): sort_order = jnp.argsort(dest_group * n_pairs + jnp.arange(n_pairs))]
  transfers between devices with their start and end apart: 9 -> 0, of which waited for: 5 -> 0; matrix products, arithmetic and copies ran while one was open for 65% -> 0% of each run, Pallas kernels for 0% -> 0%
where the time goes in v1:
time: 104 us; the launch traced here: 103 us
  Pallas kernels  101 us (97%)
  local copies, waits for them, and re-layouts  2.26 us (2%)
    pallas_call x1, Pallas kernels, device_body(): pl.pallas_call(layer_kernel, out_shape=jax.ShapeDtypeStruct((rows, width)...  101 us
    unnamed x1, local copies, waits for them, and re-layouts  2.26 us

profile of v1, /device:TPU:0, one launch (start us, length us, event | category | flops | bytes accessed | tf_op | source)
XLA Modules:
  0.0 103.5 jit_solution(8964404351312980020)
XLA Ops:
  0.0 101.2 %moe_layer.1 = bf16[512,1024]{1,0:T(8,128)(2,1)} custom-call(bf16[512,1024]{1,0:T(8,128)(2,1)} %h_ref.1, s32[8,512]{1,0:T(8,128)} %bitcast.10, f32[8,512]{1,0:T(8,128)} %bitcast.11, s32[1,512]{1,0:T(1,128)} %bitcast.13, f32[1,1024]{1,0:T(1,128)} %bitcast.12, bf16[512,256,256]{2,1,0:T(8,128)(2,1)} %bitcast.5.k_hbm, bf16[512,256,256]{2,1,0:T(8,128)(2,1)} %bitcast.7.v_hbm, ...), custom_call_target="tpu_custom_call" | custom-call | tf_op jit(solution)/shard_map/moe_layer/pallas_call | solution.py:344
  101.2 2.3 %copy.19 = bf16[512,1024]{1,0:T(8,128)(2,1)} copy(bf16[512,1024]{1,0:T(8,128)(2,1)} %moe_layer.1) | data formatting | bytes 2097152

commit v2 on v1

v2 whole, which is shorter than its diff:
```python
import functools

import jax
import jax.numpy as jnp
from jax import lax
from jax.experimental import pallas as pl
from jax.experimental.pallas import tpu as pltpu
from jax.sharding import PartitionSpec as P

NORM_EPS = 1e-6
F32 = jnp.float32
BF16 = jnp.bfloat16
MESH = pl.DeviceIdType.MESH

BLK = 16
SLOTS = 4
CHUNK = 64
LAG = 4
HEAD_BLOCKS = 8


def layer_kernel(
    h_ref, ids_ref, gates_ref, lens_ref, gain_ref, k_hbm, v_hbm, wq_hbm, wk_hbm, wv_hbm, wo_hbm, wsg_hbm, wsu_hbm, wsd_hbm,
    weg_hbm, weu_hbm, wed_hbm,
    out_hbm,
    wq, wk, wv, wo, wsg, wsu, wsd, weg, weu, wed, kbuf, vbuf,
    h_in, ids_in, gates_in, xs, aug, qdiag, heads, vflip, acc, dpart, cwb,
    psend, precv, dsend, drecv, xsend, xrecv, ysend, yrecv,
    wsem, wosem, esem, ksem, vsem, hs_send, hs_recv, p_send, p_recv, d_send, d_recv, x_send, x_recv, y_send, y_recv, osem,
):
    tp = lax.axis_index("tp")
    ep = lax.axis_index("ep")
    dp = lax.axis_index("dp")
    core = lax.rem(ep, 2)
    chip = ep // 2
    partner = (dp, tp, 2 * chip + 1 - core)
    xnbr = (dp, tp, 2 * (1 - chip) + core)
    ynbr = (dp, 1 - tp, ep)

    rows = h_ref.shape[0]
    n_blocks = rows // BLK
    n_chunks = rows // CHUNK
    kv_width = wk.shape[1]
    n_local = weg.shape[0]
    n_heads = wq.shape[1] // 64
    seq_len = kbuf.shape[3]

    small = [(wq_hbm, wq), (wk_hbm, wk), (wv_hbm, wv), (wsg_hbm, wsg), (wsu_hbm, wsu), (wsd_hbm, wsd)]
    small_copies = [pltpu.make_async_copy(s, d, wsem.at[i]) for i, (s, d) in enumerate(small)]
    for c in small_copies:
        c.start()
    barrier = pltpu.get_barrier_semaphore()
    for dev in (partner, xnbr, ynbr):
        pl.semaphore_signal(barrier, inc=1, device_id=dev, device_id_type=MESH)
    big_copies = [pltpu.make_async_copy(s, d, esem.at[i]) for i, (s, d) in enumerate(((weg_hbm, weg), (weu_hbm, weu), (wed_hbm, wed)))]
    for c in big_copies:
        c.start()
    def remote(src, dst, ssem, rsem, dev):
        return pltpu.make_async_remote_copy(src_ref=src, dst_ref=dst, send_sem=ssem, recv_sem=rsem, device_id=dev, device_id_type=MESH)

    def half_rows(m):
        return pl.ds(pl.multiple_of(m * (rows // 2), rows // 2), rows // 2)

    def row_copy(src, slot, m, dev):
        return remote(src.at[half_rows(m)], h_in.at[slot, half_rows(m)], hs_send.at[slot, m], hs_recv.at[slot, m], dev)

    def route_copies(ids, gates, slot, dev):
        pairs = ((ids, ids_in.at[slot]), (gates, gates_in.at[slot]))
        return [remote(s, d, hs_send.at[slot, 2 + i], hs_recv.at[slot, 2 + i], dev) for i, (s, d) in enumerate(pairs)]

    routes = [
        route_copies(ids_ref, gates_ref, 0, partner),
        route_copies(ids_ref, gates_ref, 1, xnbr),
        route_copies(ids_in.at[1], gates_in.at[1], 2, partner),
    ]

    def rows_to_partner(m):
        return row_copy(h_ref, 0, m, partner)

    def rows_to_xnbr(m):
        return row_copy(h_ref, 1, m, xnbr)

    def rows_forward(m):
        return row_copy(h_in.at[1], 2, m, partner)

    wo_copies = []
    for i in range(n_heads):
        dst_row = (i % 2) * kv_width + (i // 2) * 64
        wo_copies.append(pltpu.make_async_copy(wo_hbm.at[pl.ds(i * 64, 64), :], wo.at[pl.ds(dst_row, 64), :], wosem.at[i]))

    def kv_copies(b, slot):
        start = pl.multiple_of(b * BLK, BLK)
        return (
            pltpu.make_async_copy(k_hbm.at[pl.ds(start, BLK)], kbuf.at[slot], ksem.at[slot]),
            pltpu.make_async_copy(v_hbm.at[pl.ds(start, BLK)], vbuf.at[slot], vsem.at[slot]),
        )

    half = rows // 2

    def normalize(src, m):
        for i in range(half // 64):
            hf = src[pl.ds(m * half + i * 64, 64), :].astype(F32)
            inv = lax.rsqrt(jnp.mean(hf * hf, axis=1, keepdims=True) + NORM_EPS)
            xs[m, i * 64 : i * 64 + 64, :] = (hf * inv * gain_ref[...]).astype(BF16)

    def gate_weights(table, ids, gates):
        first = ep * (2 * n_local) + tp * n_local
        expert = first + lax.broadcasted_iota(jnp.int32, (8, half), 0)
        total = jnp.zeros((8, half), F32)
        for j in range(ids.shape[0]):
            total += jnp.where(ids[j : j + 1, :] == expert, gates[j : j + 1, :], 0.0)
        cols = total.T
        for e in range(n_local):
            cwb[table, e] = jnp.broadcast_to(cols[:, e : e + 1], (half, 128))

    def experts(dst, dst_row, m, table):
        d = pl.ds(dst_row, half)

        @pl.loop(0, n_local // 2)
        def _(i):
            x = xs[m]
            total = dst[d, :]
            hids = []
            for k in range(2):
                gate = jnp.dot(x, weg[2 * i + k], preferred_element_type=F32)
                up = jnp.dot(x, weu[2 * i + k], preferred_element_type=F32)
                hids.append((gate * jax.nn.sigmoid(gate) * up).astype(BF16))
            for k in range(2):
                y = jnp.dot(hids[k], wed[2 * i + k], preferred_element_type=F32)
                total = total + jnp.tile(cwb[table, 2 * i + k], (1, y.shape[1] // 128)) * y
            dst[d, :] = total

    for m in range(2):
        normalize(h_ref, m)
    for c in small_copies:
        c.wait()
    for b in range(SLOTS):
        for c in kv_copies(b, b):
            c.start()
    for c in wo_copies:
        c.start()

    col = lax.broadcasted_iota(jnp.int32, (n_heads * 64, n_heads * 64), 1)
    row = lax.broadcasted_iota(jnp.int32, (n_heads * 64, n_heads * 64), 0)
    src_row = ((lax.rem(col, kv_width) // 64) * 2 + col // kv_width) * 64 + lax.rem(col, 64)
    perm = (row == src_row).astype(F32).astype(BF16)
    lens = jnp.broadcast_to(lens_ref[...], (8, rows)).astype(F32).T
    q_w = n_heads * 64
    R8 = BLK * n_heads
    rep = (lax.broadcasted_iota(jnp.int32, (R8, BLK), 0) // n_heads == lax.broadcasted_iota(jnp.int32, (R8, BLK), 1)).astype(F32).astype(BF16)
    r_i = lax.broadcasted_iota(jnp.int32, (R8, kv_width), 0)
    c_i = lax.broadcasted_iota(jnp.int32, (R8, kv_width), 1)
    own_head = lax.rem(r_i, n_heads) // 2 == c_i // 64
    even = lax.rem(r_i, 2) == 0
    for m in range(2):
        r = pl.ds(m * half, half)
        x = xs[m]
        q = jnp.dot(x, wq[...], preferred_element_type=F32).astype(BF16)
        qp = jnp.dot(q, perm, preferred_element_type=F32).astype(BF16)
        for g in range(2):
            heads[pl.ds(g * rows + m * half, half), :] = qp[:, g * kv_width : (g + 1) * kv_width]
        aug[r, 0:kv_width] = jnp.dot(x, wk[...], preferred_element_type=F32).astype(BF16)
        aug[r, kv_width : 2 * kv_width] = jnp.dot(x, wv[...], preferred_element_type=F32).astype(BF16)
        aug[r, 2 * kv_width : 2 * kv_width + 128] = jnp.broadcast_to(lens[m * half : (m + 1) * half, 0:1], (half, 128)).astype(BF16)
        gate = jnp.dot(x, wsg[...], preferred_element_type=F32)
        up = jnp.dot(x, wsu[...], preferred_element_type=F32)
        hid = (gate * jax.nn.sigmoid(gate) * up).astype(BF16)
        acc[r, :] = jnp.dot(hid, wsd[...], preferred_element_type=F32)

    pl.semaphore_wait(barrier, 3)
    for c in routes[1] + routes[0] + [rows_to_xnbr(0), rows_to_partner(0), rows_to_xnbr(1), rows_to_partner(1)]:
        c.start()

    @pl.loop(0, n_blocks // 8)
    def _(i):
        for k in range(8):
            b = 8 * i + k
            both = [jnp.dot(rep, heads[pl.ds(pl.multiple_of(g * rows + b * BLK, BLK), BLK), :], preferred_element_type=F32) for g in range(2)]
            mine = jnp.where(even, both[0], both[1])
            qdiag[pl.ds(pl.multiple_of(b * R8, R8), R8), :] = jnp.where(own_head, mine, 0.0).astype(BF16)

    n_pairs = BLK // 2

    def attend_pair(b0):
        slots = [lax.rem(b0 + j, SLOTS) for j in range(2)]
        for j in range(2):
            for c in kv_copies(b0 + j, slots[j]):
                c.wait()
        scores, news, sums = [], [], []
        for j in range(2):
            parts = []
            for t in range(BLK):
                vflip[j, t] = vbuf[slots[j], t].T
            for p in range(n_pairs):
                lhs = qdiag[pl.ds(pl.multiple_of((b0 + j) * R8 + 16 * p, 16), 16), :]
                parts.append(jnp.dot(lhs, kbuf[slots[j], 2 * p], preferred_element_type=F32)[0:8])
                parts.append(jnp.dot(lhs, kbuf[slots[j], 2 * p + 1], preferred_element_type=F32)[8:16])
            scores.append(jnp.concatenate(parts, axis=0) * 0.125)
        for j in range(2):
            news.append(jnp.dot(rep, aug[pl.ds(pl.multiple_of((b0 + j) * BLK, BLK), BLK), :], preferred_element_type=F32))
        weights = []
        for j in range(2):
            full = news[j]
            qf = qdiag[pl.ds(pl.multiple_of((b0 + j) * R8, R8), R8), :].astype(F32)
            s_new = jnp.sum(qf * full[:, 0:kv_width], axis=1, keepdims=True) * 0.125
            ln = full[:, 2 * kv_width : 2 * kv_width + 128]
            pos = lax.broadcasted_iota(jnp.int32, (R8, seq_len), 1).astype(F32)
            s = jnp.where(pos < jnp.tile(ln, (1, seq_len // 128)), scores[j], -1e30)
            top = jnp.maximum(jnp.max(s, axis=1, keepdims=True), s_new)
            w = jnp.exp(s - top)
            w_new = jnp.exp(s_new - top)
            sums.append((w_new, jnp.sum(w, axis=1, keepdims=True) + w_new))
            weights.append(w.astype(BF16))
        for j in range(2):
            parts = []
            for p in range(n_pairs):
                lhs = weights[j][16 * p : 16 * p + 16]
                parts.append(jnp.dot(lhs, vflip[j, 2 * p], preferred_element_type=F32)[0:8])
                parts.append(jnp.dot(lhs, vflip[j, 2 * p + 1], preferred_element_type=F32)[8:16])
            w_new, den = sums[j]
            num = jnp.concatenate(parts, axis=0) + w_new * news[j][:, kv_width : 2 * kv_width]
            heads[pl.ds(pl.multiple_of((b0 + j) * R8, R8), R8), :] = jnp.where(own_head, num / den, 0.0).astype(BF16)

    def attend_blocks(first, count):
        @pl.loop(0, count // 2)
        def _(i):
            b = first + 2 * i
            attend_pair(b)

            @pl.when(b + SLOTS < n_blocks)
            def _():
                for j in range(2):
                    for c in kv_copies(b + j + SLOTS, lax.rem(b + j, SLOTS)):
                        c.start()

    def half_copy(src, dst, ssem, rsem, m):
        r = pl.ds(m * half, half)
        return remote(src.at[r, :], dst.at[r, :], ssem.at[m], rsem.at[m], partner)

    def wait_recv(copies):
        for c in copies:
            c.wait_recv()

    for c in big_copies:
        c.wait()

    @pl.loop(0, 2)
    def _(m):
        gate_weights(0, ids_ref[:, half_rows(m)], gates_ref[:, half_rows(m)])
        experts(acc, m * half, m, 0)
        attend_blocks(4 * m, 4)

    for c in routes[1]:
        c.wait_recv()
    for c in routes[2]:
        c.start()
    for c in routes[0] + routes[2]:
        c.wait_recv()

    def chunk_copy(src, dst, ssem, rsem, c, dev):
        r = pl.ds(pl.multiple_of(c * CHUNK, CHUNK), CHUNK)
        return remote(src.at[r, :], dst.at[r, :], ssem.at[c], rsem.at[c], dev)

    for c in wo_copies:
        c.wait()

    def out_copy(c):
        r = pl.ds(pl.multiple_of(c * CHUNK, CHUNK), CHUNK)
        q = pl.ds(pl.multiple_of(lax.rem(c, n_chunks // 2) * CHUNK, CHUNK), CHUNK)
        return pltpu.make_async_copy(xs.at[c // (n_chunks // 2), q, :], out_hbm.at[r, :], osem.at[c])

    def finish(c):
        r = pl.ds(pl.multiple_of(c * CHUNK, CHUNK), CHUNK)
        chunk_copy(ysend, yrecv, y_send, y_recv, c, ynbr).wait_recv()
        both = ysend[r, :].astype(F32) + yrecv[r, :].astype(F32)
        q = pl.ds(pl.multiple_of(lax.rem(c, n_chunks // 2) * CHUNK, CHUNK), CHUNK)
        xs[c // (n_chunks // 2), q, :] = (h_ref[r, :].astype(F32) + both).astype(BF16)
        out_copy(c).start()

    rows_c = CHUNK * n_heads
    g_r = lax.broadcasted_iota(jnp.int32, (2 * CHUNK, rows_c), 0)
    g_c = lax.broadcasted_iota(jnp.int32, (2 * CHUNK, rows_c), 1)
    fold = ((g_c // n_heads == lax.rem(g_r, CHUNK)) & (lax.rem(g_c, 2) == g_r // CHUNK)).astype(F32).astype(BF16)

    def combine(c):
        r = pl.ds(pl.multiple_of(c * CHUNK, CHUNK), CHUNK)
        o = jnp.dot(fold, heads[pl.ds(pl.multiple_of(c * rows_c, rows_c), rows_c), :], preferred_element_type=F32).astype(BF16)
        attn = jnp.dot(o[0:CHUNK], wo[0:kv_width, :], preferred_element_type=F32) + jnp.dot(o[CHUNK : 2 * CHUNK], wo[kv_width : 2 * kv_width, :], preferred_element_type=F32)
        chunk_copy(xsend, xrecv, x_send, x_recv, c, xnbr).wait_recv()
        ysend[r, :] = (acc[r, :] + attn + precv[r, :].astype(F32) + xrecv[r, :].astype(F32)).astype(BF16)
        chunk_copy(ysend, yrecv, y_send, y_recv, c, ynbr).start()

    def remote_unit(slot, m, table):
        gate_weights(table, ids_in[slot, :, half_rows(m)], gates_in[slot, :, half_rows(m)])
        normalize(h_in.at[slot], m)
        dpart[...] = jnp.zeros_like(dpart)
        experts(dpart, 0, m, table)

    first_chunks = n_chunks // 2

    @pl.loop(0, 2)
    def _(m):
        r = half_rows(m)
        b = HEAD_BLOCKS + 8 * m

        def early(c):
            @pl.when(m == 1)
            def _():
                if c == 0:
                    half_copy(psend, precv, p_send, p_recv, 0).wait_recv()
                combine(c)

        rows_to_xnbr(m).wait_recv()
        rows_forward(m).start()
        attend_blocks(b, 2)
        early(0)
        rows_forward(m).wait_recv()
        remote_unit(2, m, 0)
        dsend[r, :] = dpart[...].astype(BF16)
        half_copy(dsend, drecv, d_send, d_recv, m).start()
        early(1)
        attend_blocks(b + 2, 2)
        early(2)
        remote_unit(1, m, 1)
        half_copy(dsend, drecv, d_send, d_recv, m).wait_recv()
        xsend[r, :] = (dpart[...] + drecv[r, :].astype(F32)).astype(BF16)
        for i in range(first_chunks):
            chunk_copy(xsend, xrecv, x_send, x_recv, m * first_chunks + i, xnbr).start()
        attend_blocks(b + 4, 2)
        early(3)
        rows_to_partner(m).wait_recv()
        remote_unit(0, m, 2)
        psend[r, :] = dpart[...].astype(BF16)
        half_copy(psend, precv, p_send, p_recv, m).start()
        attend_blocks(b + 6, 2)

    half_copy(psend, precv, p_send, p_recv, 1).wait_recv()

    @pl.loop(first_chunks, n_chunks)
    def _(c):
        attend_blocks(HEAD_BLOCKS + 16 + 2 * (c - first_chunks), 2)
        combine(c)
        finish(c - LAG)

    for c in range(n_chunks - LAG, n_chunks):
        finish(c)

    for c in routes[0] + routes[1] + routes[2]:
        c.wait_send()
    for m in range(2):
        for c in (rows_to_partner(m), rows_to_xnbr(m), rows_forward(m)):
            c.wait_send()
        half_copy(psend, precv, p_send, p_recv, m).wait_send()
        half_copy(dsend, drecv, d_send, d_recv, m).wait_send()

    @pl.loop(0, n_chunks)
    def _(c):
        r = pl.ds(pl.multiple_of(c * CHUNK, CHUNK), CHUNK)
        chunk_copy(xsend, xrecv, x_send, x_recv, c, xnbr).wait_send()
        chunk_copy(ysend, yrecv, y_send, y_recv, c, ynbr).wait_send()
        out_copy(c).wait()


def solution(mesh):
    tok_rows = P(("dp", "ep"), None)
    cache_spec = P(("dp", "ep"), None, "tp", None)
    col_split = P(None, "tp")
    row_split = P("tp", None)
    exp_split = P(("ep", "tp"), None, None)
    in_specs = (tok_rows, cache_spec, cache_spec, P(("dp", "ep")), tok_rows, tok_rows, P(None), col_split, col_split, col_split, row_split, col_split, col_split, row_split, exp_split, exp_split, exp_split)

    def device_body(hidden, k_cache, v_cache, lengths, expert_ids, route_gates, norm_gain, w_query, w_key, w_value, w_out, ws_gate, ws_up, ws_down, we_gate, we_up, we_down):
        rows, width = hidden.shape
        seq_len, kv_local, head_dim = k_cache.shape[1:]
        kv_width = kv_local * head_dim
        top_k = expert_ids.shape[1]
        k_t = k_cache.transpose(0, 2, 3, 1).reshape(rows, kv_width, seq_len)
        v_t = v_cache.transpose(0, 2, 3, 1).reshape(rows, kv_width, seq_len)
        n_chunks = rows // CHUNK
        q_w = w_query.shape[1]
        dma = pltpu.SemaphoreType.DMA
        vmem = pltpu.VMEM
        scratch = [
            vmem(w_query.shape, BF16), vmem(w_key.shape, BF16), vmem(w_value.shape, BF16), vmem(w_out.shape, BF16),
            vmem(ws_gate.shape, BF16), vmem(ws_up.shape, BF16), vmem(ws_down.shape, BF16),
            vmem(we_gate.shape, BF16), vmem(we_up.shape, BF16), vmem(we_down.shape, BF16),
            vmem((SLOTS, BLK, kv_width, seq_len), BF16), vmem((SLOTS, BLK, kv_width, seq_len), BF16),
            vmem((3, rows, width), BF16), vmem((3, top_k, rows), jnp.int32), vmem((3, top_k, rows), F32),
            vmem((2, rows // 2, width), BF16), vmem((rows, 2 * kv_width + 128), BF16),
            vmem((rows * q_w // head_dim, kv_width), BF16), vmem((rows * q_w // head_dim, kv_width), BF16),
            vmem((2, BLK, seq_len, kv_width), BF16),
            vmem((rows, width), F32), vmem((rows // 2, width), F32), vmem((3, we_gate.shape[0], rows // 2, 128), F32),
            vmem((rows, width), BF16), vmem((rows, width), BF16), vmem((rows, width), BF16), vmem((rows, width), BF16),
            vmem((rows, width), BF16), vmem((rows, width), BF16), vmem((rows, width), BF16), vmem((rows, width), BF16),
            dma((6,)), dma((q_w // head_dim,)), dma((3,)), dma((SLOTS,)), dma((SLOTS,)),
            dma((3, 4)), dma((3, 4)), dma((2,)), dma((2,)), dma((2,)), dma((2,)),
            dma((n_chunks,)), dma((n_chunks,)), dma((n_chunks,)), dma((n_chunks,)), dma((n_chunks,)),
        ]
        in_vmem = pl.BlockSpec(memory_space=pltpu.VMEM)
        anywhere = pl.BlockSpec(memory_space=pl.ANY)
        return pl.pallas_call(
            layer_kernel,
            out_shape=jax.ShapeDtypeStruct((rows, width), BF16),
            in_specs=[in_vmem] * 5 + [anywhere] * 12,
            out_specs=anywhere,
            scratch_shapes=scratch,
            compiler_params=pltpu.CompilerParams(collective_id=0, has_side_effects=True, vmem_limit_bytes=67043328),
            name="moe_layer",
        )(hidden, expert_ids.T, route_gates.T, lengths.reshape(1, rows), norm_gain.reshape(1, width), k_t, v_t, w_query, w_key, w_value, w_out, ws_gate, ws_up, ws_down, we_gate, we_up, we_down)

    return jax.shard_map(device_body, mesh=mesh, in_specs=in_specs, out_specs=tok_rows, check_vma=False)
```

time: 104 us -> 84.4 us (0.81)
  Pallas kernels: 101 us -> 82 us
    pallas_call x1, Pallas kernels: 101 us -> 82 us  [device_body(): pl.pallas_call(layer_kernel, out_shape=jax.ShapeDtypeStruct((rows, width)...]
where the time goes in v2:
time: 84.4 us; the launch traced here: 84.2 us
  Pallas kernels  82 us (97%)
  local copies, waits for them, and re-layouts  2.26 us (3%)
    pallas_call x1, Pallas kernels, device_body(): pl.pallas_call(layer_kernel, out_shape=jax.ShapeDtypeStruct((rows, width)...  82 us
    unnamed x1, local copies, waits for them, and re-layouts  2.26 us

profile of v2, /device:TPU:0, one launch (start us, length us, event | category | flops | bytes accessed | tf_op | source)
XLA Modules:
  0.0 84.2 jit_solution(15610825835038708675)
XLA Ops:
  0.0 82.0 %moe_layer.1 = bf16[512,1024]{1,0:T(8,128)(2,1)} custom-call(bf16[512,1024]{1,0:T(8,128)(2,1)} %h_ref.1, s32[8,512]{1,0:T(8,128)} %bitcast.10, f32[8,512]{1,0:T(8,128)} %bitcast.11, s32[1,512]{1,0:T(1,128)} %bitcast.13, f32[1,1024]{1,0:T(1,128)} %bitcast.12, bf16[512,256,256]{2,1,0:T(8,128)(2,1)} %bitcast.5.k_hbm, bf16[512,256,256]{2,1,0:T(8,128)(2,1)} %bitcast.7.v_hbm, ...), custom_call_target="tpu_custom_call" | custom-call | tf_op jit(solution)/shard_map/moe_layer/pallas_call | solution.py:401
  82.0 2.3 %copy.19 = bf16[512,1024]{1,0:T(8,128)(2,1)} copy(bf16[512,1024]{1,0:T(8,128)(2,1)} %moe_layer.1) | data formatting | bytes 2097152
